TPU v7x, 32 devices: a whole 2x2x4 slice. The times are simulated.
32 devices in a mesh: groups: 2 (over x), blk: 8 (over z, y), span: 2 (over core).
Axes of the slice: x: 2, y: 2, z: 4, core: 2. Of those that a mesh axis runs over, the one named last changes fastest.
Arguments:
- embeddings: bfloat16 [8192, 768], P(('groups', 'blk', 'span')), parts along dimension 0, may hold values from -6 to 6
- owner_ids: int32 [8192, 1], P(('groups', 'blk', 'span')), parts along dimension 0, may hold values from 0 to 7, as said below
- local_ids: int32 [8192], P(('groups', 'blk', 'span')), parts along dimension 0, may hold values from 0 to 15, as said below
- cluster_map: int32 [256], P('groups'), parts along dimension 0, may hold values from 0 to 127, as said below
Outputs:
- nearest: float32 [8192], P(('groups', 'blk', 'span')), parts along dimension 0
- centroid_cosine: float32 [8192], P(('groups', 'blk', 'span')), parts along dimension 0
There are 2 independent parts, one for each index of `groups`. A program takes and returns all parts, laid end to end along the dimension named above; each array names one. Nothing has to cross between parts.
Inputs may be any that keep to these rules, and one draw needn't show every extreme that they name: `owner_ids`: at most 64 rows of one device name the same owner; in every draw one owner is named by exactly 64 rows of every device. `local_ids`: of the rows of one device that name one owner, at most 16 have local id 0; in every draw one owner receives exactly 16 rows with local id 0 from every device. In every draw some clusters with a local id other than 0 have exactly one row in the whole shard. cluster_map[o * 16 + l] = o * 16 + l for l > 0. For l = 0 the owners fall into runs of 1 to 3 consecutive owners, and every owner of a run has the value of the run's first owner; some run has 3 owners.
All inputs are finite; a program needn't handle non-finite values.
Results may differ from a plain program's by a relative error of at most 0.0017.
Values may be sent and summed in bfloat16 or wider, within the bound.
No kernel may reach another device: no remote copies, remote signals or barrier semaphores. Data moves between devices by JAX's collectives and lax.ppermute only.
A program may use at most 64 MiB of HBM per device.

v0:
```python
import jax
import jax.numpy as jnp
from jax import lax
from jax.sharding import PartitionSpec as P

GIANT_SPAN = 3


def passed_along(value, axis, steps):
    count = lax.axis_size(axis)
    first, last = (max(0, -steps), min(count, count - steps))
    return lax.ppermute(value, axis, [(source, source + steps) for source in range(first, last)])


def normalize(values):
    wide = values.astype(jnp.float32)
    scale = lax.rsqrt(jnp.sum(wide * wide, axis=1, keepdims=True) + 1e-06)
    return (wide * scale).astype(jnp.bfloat16)


def masked_scores(left, left_tags, right, right_tags):
    scores = lax.dot_general(
        left, right, (((1,), (1,)), ((), ())), preferred_element_type=jnp.float32
    )
    same = (left_tags[:, None] == right_tags[None, :]) & (left_tags[:, None] > 0)
    return jnp.where(same, scores, -1.0)


def body(embeddings, owner_ids, local_ids, cluster_map):
    rows = embeddings.shape[0]
    width = embeddings.shape[1]
    owners = lax.axis_size("blk")
    capacity = 2 * rows // owners
    slots = owners * capacity
    clusters = cluster_map.shape[0]
    owned = clusters // owners
    unit = normalize(embeddings)
    destination = owner_ids[:, 0]
    flat = destination * owned + local_ids
    table = jnp.arange(clusters, dtype=jnp.int32)
    cluster = jnp.sum(jnp.where(flat[:, None] == table[None, :], cluster_map[None, :], 0), axis=1)
    onehot = (destination[:, None] == jnp.arange(owners, dtype=jnp.int32)[None, :]).astype(
        jnp.int32
    )
    before = jnp.cumsum(onehot, axis=0) - onehot
    rank = jnp.sum(before * onehot, axis=1)
    position = destination * capacity + rank
    send_rows = jnp.zeros((slots, width), jnp.bfloat16).at[position].set(unit)
    send_tags = jnp.zeros((slots,), jnp.int32).at[position].set(cluster + 1)
    arrived, arrived_tags = (
        lax.all_to_all(
            send_rows.reshape(owners, capacity, width),
            "blk",
            split_axis=0,
            concat_axis=0,
            tiled=True,
        ),
        lax.all_to_all(
            send_tags.reshape(owners, capacity), "blk", split_axis=0, concat_axis=0, tiled=True
        ),
    )
    mine = arrived.reshape(slots, width)
    my_tags = arrived_tags.reshape(slots)
    chip, chip_tags = (
        lax.all_gather(mine, "span", axis=0, tiled=True),
        lax.all_gather(my_tags, "span", axis=0, tiled=True),
    )
    half = lax.axis_index("span")
    block_index = lax.axis_index("blk")
    own_tags = lax.dynamic_slice_in_dim(cluster_map, block_index * owned, owned, 0) + 1
    local = masked_scores(mine, my_tags, chip, chip_tags)
    itself = (
        jnp.arange(2 * slots, dtype=jnp.int32)[None, :]
        == (jnp.arange(slots, dtype=jnp.int32) + half * slots)[:, None]
    )
    best = jnp.max(jnp.where(itself, -1.0, local), axis=1)
    share_limit = 2 * owners * max(1, capacity // 4)
    shared_mask = chip_tags == own_tags[0]
    packed_rank = jnp.cumsum(shared_mask.astype(jnp.int32)) - 1
    target = jnp.where(shared_mask, packed_rank, share_limit)
    packed = jnp.zeros((share_limit, width), jnp.bfloat16).at[target].set(chip, mode="drop")
    packed_tags = jnp.zeros((share_limit,), jnp.int32).at[target].set(chip_tags, mode="drop")
    upper = (packed, packed_tags)
    lower = (packed, packed_tags)
    for step in range(1, GIANT_SPAN):
        upper = passed_along((upper[0], upper[1]), "blk", 1)
        lower = passed_along((lower[0], lower[1]), "blk", -1)
        for other in (upper, lower):
            best = jnp.maximum(
                best, jnp.max(masked_scores(mine, my_tags, other[0], other[1]), axis=1)
            )
    chosen = cluster[:, None] == table[None, :]
    partial_sums = lax.dot_general(
        chosen.astype(jnp.bfloat16),
        unit,
        (((0,), (0,)), ((), ())),
        preferred_element_type=jnp.float32,
    )
    sums = lax.psum(partial_sums, ("blk", "span"))
    length = jnp.sqrt(jnp.sum(sums * sums, axis=1, keepdims=True))
    direction = sums / jnp.maximum(length, 1.0)
    centroid_cosine = jnp.sum(unit.astype(jnp.float32) * direction[cluster], axis=1)
    returned_best = lax.all_to_all(
        best.reshape(owners, capacity), "blk", split_axis=0, concat_axis=0, tiled=True
    )
    nearest = returned_best.reshape(slots)[position]
    return (nearest, centroid_cosine)


def solution(mesh):
    return jax.shard_map(
        body,
        mesh=mesh,
        in_specs=(
            P(("groups", "blk", "span"), None),
            P(("groups", "blk", "span"), None),
            P(("groups", "blk", "span")),
            P("groups"),
        ),
        out_specs=(P(("groups", "blk", "span")), P(("groups", "blk", "span"))),
        check_vma=False,
    )
```

profile of v0, /device:TPU:0, one launch (start us, length us, event | category | flops | bytes accessed | tf_op | source)
XLA Modules:
  0.0 191.0 jit_solution(9322189716579336675)
XLA Ops:
  8.0 1.2 fusion
  10.8 0.8 fusion.9
  12.2 3.1 %scatter_custom_fusion.1 = bf16[512,768]{1,0:T(8,128)(2,1)} fusion(s32[256]{0:T(256)S(1)} %bitcast.54, bf16[]{:T(256)} %constant.23.clone.1, bf16[256,768]{1,0:T(8,128)(2,1)} %param.4, f32[256]{0:T(256)S(1)} %add_rsqrt_fusion), kind=kCustom, calls=%fused_computation.18 | custom fusion | flops 589824 | bytes 1180674 | tf_op jit(solution)/shard_map/scatter | solution.py:48
  15.3 7.3 %all-to-all-start.1 = ((bf16[8,64,768]{2,1,0:T(8,128)(2,1)}), bf16[8,64,768]{2,1,0:T(8,128)(2,1)S(1)}, u32[]{:S(2)}, u32[]{:S(2)}) async-start(bf16[8,64,768]{2,1,0:T(8,128)(2,1)} %bitcast.7), calls=%async_computation.1 | async-start | bytes 1572864 | tf_op jit(solution)/shard_map/all_to_all | solution.py:51
  22.9 1.1 fusion.6
  24.1 1.4 scatter_custom_fusion
  26.7 16.9 %all-to-all-done.1 = bf16[8,64,768]{2,1,0:T(8,128)(2,1)S(1)} async-done(((bf16[8,64,768]{2,1,0:T(8,128)(2,1)}), bf16[8,64,768]{2,1,0:T(8,128)(2,1)S(1)}, u32[]{:S(2)}, u32[]{:S(2)}) %all-to-all-start.1) | async-done | bytes 786464 | tf_op jit(solution)/shard_map/all_to_all | solution.py:51
  43.6 3.5 %all-to-all-start = ((s32[8,1,64]{2,1,0:T(1,128)}), s32[8,1,64]{2,1,0:T(1,128)S(1)}, u32[]{:S(2)}, u32[]{:S(2)}) async-start(s32[8,1,64]{2,1,0:T(1,128)} %all_to_all.13), calls=%async_computation | async-start | bytes 8192 | tf_op jit(solution)/shard_map/all_to_all | solution.py:58
  48.3 5.2 %all-to-all-done = s32[8,1,64]{2,1,0:T(1,128)S(1)} async-done(((s32[8,1,64]{2,1,0:T(1,128)}), s32[8,1,64]{2,1,0:T(1,128)S(1)}, u32[]{:S(2)}, u32[]{:S(2)}) %all-to-all-start) | async-done | bytes 2080 | tf_op jit(solution)/shard_map/all_to_all | solution.py:58
  53.7 1.8 all-gather
  56.1 4.3 %scatter_custom_fusion.2 = s32[256]{0:T(256)S(1)} fusion(s32[1024]{0:T(1024)S(1)} %compare_select_fusion, s32[1024]{0:T(1024)S(1)} %bitcast.49, s32[]{:T(128)} %constant.19.clone.1), kind=kCustom, calls=%fused_computation.53 | custom fusion | bytes 1028 | tf_op jit(solution)/shard_map/scatter | solution.py:82
  60.4 1.3 collective-permute-start.2
  61.7 5.1 %collective-permute-start = (s32[256]{0:T(256)S(1)}, s32[256]{0:T(256)}, u32[]{:S(2)}, u32[]{:S(2)}) collective-permute-start(s32[256]{0:T(256)S(1)} %scatter_custom_fusion.2), channel_id=1, source_target_pairs={{0,2},{2,4},{4,6},{6,8},{8,10},{10,12},{12,14},{1,3},{3,5},{5,7},{... | collective-permute-start | bytes 3080 | tf_op jit(solution)/shard_map/ppermute | solution.py:12
  68.6 1.3 collective-permute-start.6
  69.9 5.1 %collective-permute-start.4 = (s32[256]{0:T(256)}, s32[256]{0:T(256)}, u32[]{:S(2)}, u32[]{:S(2)}) collective-permute-start(s32[256]{0:T(256)} %collective-permute-done), channel_id=1, source_target_pairs={{0,2},{2,4},{4,6},{6,8},{8,10},{10,12},{12,14},{1,3},{3,5},{5,7},{... | collective-permute-start | bytes 3080 | tf_op jit(solution)/shard_map/ppermute | solution.py:12
  75.0 47.2 %all-reduce.2.cloned.1.call-done = f32[128,768]{1,0:T(8,128)} async-done(((f32[128,768]{1,0:T(8,128)}), f32[128,768]{1,0:T(8,128)}) %all-reduce.2.cloned.1.call-update) | async-done | bytes 393232 | tf_op jit(solution)/shard_map/psum | solution.py:99
  122.2 1.1 multiply_reduce_fusion.1
  123.4 5.7 %scatter_custom_fusion.3 = bf16[256,768]{1,0:T(8,128)(2,1)S(1)} fusion(s32[1024]{0:T(1024)S(1)} %compare_select_fusion, bf16[1024,768]{1,0:T(8,128)(2,1)} %all-gather.3.cloned.1.call-done, bf16[]{:T(256)} %constant.23.clone.1), kind=kCustom, calls=%fused_computation.21 | custom fusion | bytes 393728 | tf_op jit(solution)/shard_map/scatter | solution.py:81
  129.1 1.3 collective-permute-start.3
  130.4 4.6 %collective-permute-start.1 = (bf16[256,768]{1,0:T(8,128)(2,1)S(1)}, bf16[256,768]{1,0:T(8,128)(2,1)S(1)}, u32[]{:S(2)}, u32[]{:S(2)}) collective-permute-start(bf16[256,768]{1,0:T(8,128)(2,1)S(1)} %scatter_custom_fusion.3), channel_id=1, source_target_pairs={{0,2},{2,4},{4,6},{6,8},{8,10},{10,12},{12,14},{1,3},{3,5},{5,7},{... | collective-permute-start | bytes 1179656 | tf_op jit(solution)/shard_map/ppermute | solution.py:12
  135.0 1.1 broadcast_divide_fusion
  136.1 1.4 gather_fusion.1
  137.5 2.8 %select_reduce_fusion = f32[512]{0:T(512)S(1)} fusion(bf16[512,768]{1,0:T(8,128)(2,1)S(1)} %bitcast.41, bf16[1024,768]{1,0:T(8,128)(2,1)} %all-gather.3.cloned.1.call-done, s32[1024]{0:T(1024)S(1)} %bitcast.50, s32[512]{0:T(512)} %iota_add_fusion, s32[512]{0:T(512)S(1)} %eq.145, pred[512]{0:T(512)(128)(4,1)} %broadcast_compare_fusion.1), kind=kOutput, calls=%fused_computation.6 | convolution fusion | flops 808451584 | bytes 2370048 | tf_op jit(solution)/shard_map/dot_general | solution.py:22
  141.0 1.3 collective-permute-start.7
  142.3 6.2 %collective-permute-done.1 = bf16[256,768]{1,0:T(8,128)(2,1)S(1)} collective-permute-done((bf16[256,768]{1,0:T(8,128)(2,1)S(1)}, bf16[256,768]{1,0:T(8,128)(2,1)S(1)}, u32[]{:S(2)}, u32[]{:S(2)}) %collective-permute-start.1) | collective-permute-done | bytes 393248 | tf_op jit(solution)/shard_map/ppermute | solution.py:12
  148.5 4.4 %collective-permute-start.5 = (bf16[256,768]{1,0:T(8,128)(2,1)S(1)}, bf16[256,768]{1,0:T(8,128)(2,1)S(1)}, u32[]{:S(2)}, u32[]{:S(2)}) collective-permute-start(bf16[256,768]{1,0:T(8,128)(2,1)S(1)} %collective-permute-done.1), channel_id=1, source_target_pairs={{0,2},{2,4},{4,6},{6,8},{8,10},{10,12},{12,14},{1,3},{3,5},{5,7},{... | collective-permute-start | bytes 1179656 | tf_op jit(solution)/shard_map/ppermute | solution.py:12
  154.1 11.3 %collective-permute-done.5 = bf16[256,768]{1,0:T(8,128)(2,1)S(1)} collective-permute-done((bf16[256,768]{1,0:T(8,128)(2,1)S(1)}, bf16[256,768]{1,0:T(8,128)(2,1)S(1)}, u32[]{:S(2)}, u32[]{:S(2)}) %collective-permute-start.5) | collective-permute-done | bytes 393248 | tf_op jit(solution)/shard_map/ppermute | solution.py:12
  165.4 1.3 select_reduce_fusion.4
  167.4 5.9 %all-to-all-start.2 = ((f32[8,1,64]{2,1,0:T(1,128)}), f32[8,1,64]{2,1,0:T(1,128)S(1)}, u32[]{:S(2)}, u32[]{:S(2)}) async-start(f32[8,1,64]{2,1,0:T(1,128)} %max.65), calls=%async_computation.2 | async-start | bytes 8192 | tf_op jit(solution)/shard_map/all_to_all | solution.py:103
  173.3 0.8 multiply_reduce_fusion
  174.1 5.7 %all-to-all-done.2 = f32[8,1,64]{2,1,0:T(1,128)S(1)} async-done(((f32[8,1,64]{2,1,0:T(1,128)}), f32[8,1,64]{2,1,0:T(1,128)S(1)}, u32[]{:S(2)}, u32[]{:S(2)}) %all-to-all-start.2) | async-done | bytes 2080 | tf_op jit(solution)/shard_map/all_to_all | solution.py:103
  181.1 2.5 %gather_fusion = f32[256]{0:T(256)} fusion(f32[512]{0:T(512)S(1)} %reshape.165, s32[1024]{0:T(1024)S(1)} %pad_clamp_fusion.1), kind=kCustom, calls=%fused_computation | custom fusion | bytes 3072 | tf_op jit(solution)/shard_map/gather | solution.py:106
  (61 shorter events, 11.3 us)
Async XLA Ops:
  8.0 14.9 %copy-start.2 = (bf16[256,768]{1,0:T(8,128)(2,1)S(1)}, bf16[256,768]{1,0:T(8,128)(2,1)}, u32[]{:S(2)}) copy-start(bf16[256,768]{1,0:T(8,128)(2,1)} %param.4) | copy-start | bytes 1179652
  8.0 14.7 %copy-start.3 = (s32[256,1]{0,1:T(1,128)S(1)}, s32[256,1]{0,1:T(1,128)}, u32[]{:S(2)}) copy-start(s32[256,1]{0,1:T(1,128)} %param.5) | copy-start | bytes 3076
  8.0 14.7 %copy-start.4 = (s32[256]{0:T(256)S(1)}, s32[256]{0:T(256)}, u32[]{:S(2)}) copy-start(s32[256]{0:T(256)} %param.6) | copy-start | bytes 3076
  8.0 14.7 %copy-start.5 = (s32[128]{0:T(128)S(1)}, s32[128]{0:T(128)}, u32[]{:S(2)}) copy-start(s32[128]{0:T(128)} %param.7) | copy-start | bytes 1540
  15.3 28.3 %all-to-all-start.1 = ((bf16[8,64,768]{2,1,0:T(8,128)(2,1)}), bf16[8,64,768]{2,1,0:T(8,128)(2,1)S(1)}, u32[]{:S(2)}, u32[]{:S(2)}) async-start(bf16[8,64,768]{2,1,0:T(8,128)(2,1)} %bitcast.7), calls=%async_computation.1 | async-start | bytes 1572864 | tf_op jit(solution)/shard_map/all_to_all | solution.py:51
  22.6 99.6 %all-reduce.2.cloned.1.call-start = ((), (), s32[]{:S(2)}) async-start(), calls=%async_computation.4 | async-start | bytes 786432 | tf_op jit(solution)/shard_map/psum | solution.py:99
  43.6 3.5 %copy-start = (bf16[8,64,768]{2,1,0:T(8,128)(2,1)}, bf16[8,64,768]{2,1,0:T(8,128)(2,1)S(1)}, u32[]{:S(2)}) copy-start(bf16[8,64,768]{2,1,0:T(8,128)(2,1)S(1)} %all-to-all-done.1) | copy-start | bytes 2359300
  43.6 10.0 %all-to-all-start = ((s32[8,1,64]{2,1,0:T(1,128)}), s32[8,1,64]{2,1,0:T(1,128)S(1)}, u32[]{:S(2)}, u32[]{:S(2)}) async-start(s32[8,1,64]{2,1,0:T(1,128)} %all_to_all.13), calls=%async_computation | async-start | bytes 8192 | tf_op jit(solution)/shard_map/all_to_all | solution.py:58
  47.1 76.3 %all-gather.3.cloned.1.call-start = ((), (), s32[]{:S(2)}) async-start(), calls=%async_computation.3 | async-start | bytes 2359296 | tf_op jit(solution)/shard_map/all_gather | solution.py:65
  60.4 8.2 %collective-permute-start.2 = (s32[256]{0:T(256)S(1)}, s32[256]{0:T(256)}, u32[]{:S(2)}, u32[]{:S(2)}) collective-permute-start(s32[256]{0:T(256)S(1)} %scatter_custom_fusion.2), channel_id=1, source_target_pairs={{2,0},{4,2},{6,4},{8,6},{10,8},{12,10},{14,12},{3,1},{5,3},{7,5},{... | collective-permute-start | bytes 3080 | tf_op jit(solution)/shard_map/ppermute | solution.py:12
  61.7 8.2 %collective-permute-start = (s32[256]{0:T(256)S(1)}, s32[256]{0:T(256)}, u32[]{:S(2)}, u32[]{:S(2)}) collective-permute-start(s32[256]{0:T(256)S(1)} %scatter_custom_fusion.2), channel_id=1, source_target_pairs={{0,2},{2,4},{4,6},{6,8},{8,10},{10,12},{12,14},{1,3},{3,5},{5,7},{... | collective-permute-start | bytes 3080 | tf_op jit(solution)/shard_map/ppermute | solution.py:12
  68.6 85.5 %collective-permute-start.6 = (s32[256]{0:T(256)}, s32[256]{0:T(256)}, u32[]{:S(2)}, u32[]{:S(2)}) collective-permute-start(s32[256]{0:T(256)} %collective-permute-done.2), channel_id=1, source_target_pairs={{2,0},{4,2},{6,4},{8,6},{10,8},{12,10},{14,12},{3,1},{5,3},{7,5},{... | collective-permute-start | bytes 3080 | tf_op jit(solution)/shard_map/ppermute | solution.py:12
  69.9 84.3 %collective-permute-start.4 = (s32[256]{0:T(256)}, s32[256]{0:T(256)}, u32[]{:S(2)}, u32[]{:S(2)}) collective-permute-start(s32[256]{0:T(256)} %collective-permute-done), channel_id=1, source_target_pairs={{0,2},{2,4},{4,6},{6,8},{8,10},{10,12},{12,14},{1,3},{3,5},{5,7},{... | collective-permute-start | bytes 3080 | tf_op jit(solution)/shard_map/ppermute | solution.py:12
  129.1 11.9 %collective-permute-start.3 = (bf16[256,768]{1,0:T(8,128)(2,1)S(1)}, bf16[256,768]{1,0:T(8,128)(2,1)S(1)}, u32[]{:S(2)}, u32[]{:S(2)}) collective-permute-start(bf16[256,768]{1,0:T(8,128)(2,1)S(1)} %scatter_custom_fusion.3), channel_id=1, source_target_pairs={{2,0},{4,2},{6,4},{8,6},{10,8},{12,10},{14,12},{3,1},{5,3},{7,5},{... | collective-permute-start | bytes 1179656 | tf_op jit(solution)/shard_map/ppermute | solution.py:12
  130.4 18.0 %collective-permute-start.1 = (bf16[256,768]{1,0:T(8,128)(2,1)S(1)}, bf16[256,768]{1,0:T(8,128)(2,1)S(1)}, u32[]{:S(2)}, u32[]{:S(2)}) collective-permute-start(bf16[256,768]{1,0:T(8,128)(2,1)S(1)} %scatter_custom_fusion.3), channel_id=1, source_target_pairs={{0,2},{2,4},{4,6},{6,8},{8,10},{10,12},{12,14},{1,3},{3,5},{5,7},{... | collective-permute-start | bytes 1179656 | tf_op jit(solution)/shard_map/ppermute | solution.py:12
  136.1 1.4 copy-start.1
  141.0 12.7 %collective-permute-start.7 = (bf16[256,768]{1,0:T(8,128)(2,1)S(1)}, bf16[256,768]{1,0:T(8,128)(2,1)S(1)}, u32[]{:S(2)}, u32[]{:S(2)}) collective-permute-start(bf16[256,768]{1,0:T(8,128)(2,1)S(1)} %collective-permute-done.3), channel_id=1, source_target_pairs={{2,0},{4,2},{6,4},{8,6},{10,8},{12,10},{14,12},{3,1},{5,3},{7,5},{... | collective-permute-start | bytes 1179656 | tf_op jit(solution)/shard_map/ppermute | solution.py:12
  148.5 17.0 %collective-permute-start.5 = (bf16[256,768]{1,0:T(8,128)(2,1)S(1)}, bf16[256,768]{1,0:T(8,128)(2,1)S(1)}, u32[]{:S(2)}, u32[]{:S(2)}) collective-permute-start(bf16[256,768]{1,0:T(8,128)(2,1)S(1)} %collective-permute-done.1), channel_id=1, source_target_pairs={{0,2},{2,4},{4,6},{6,8},{8,10},{10,12},{12,14},{1,3},{3,5},{5,7},{... | collective-permute-start | bytes 1179656 | tf_op jit(solution)/shard_map/ppermute | solution.py:12
  153.3 12.2 %copy-start.6 = (pred[512]{0:T(512)(128)(4,1)S(1)}, pred[512]{0:T(512)(128)(4,1)}, u32[]{:S(2)}) copy-start(pred[512]{0:T(512)(128)(4,1)} %broadcast_compare_fusion.1) | copy-start | bytes 1540
  167.4 12.4 %all-to-all-start.2 = ((f32[8,1,64]{2,1,0:T(1,128)}), f32[8,1,64]{2,1,0:T(1,128)S(1)}, u32[]{:S(2)}, u32[]{:S(2)}) async-start(f32[8,1,64]{2,1,0:T(1,128)} %max.65), calls=%async_computation.2 | async-start | bytes 8192 | tf_op jit(solution)/shard_map/all_to_all | solution.py:103
Sparse Core Ops, SparseCore 0:
  26.8 95.4 all-reduce.1
Sparse Core Ops, SparseCore 1:
  49.1 11.1 all-gather.2
where the time goes:
time: 192 us; the launch traced here: 191 us
  waiting for transfers between devices  93.8 us (49%)
  starting transfers between devices  41.1 us (21%)
  local copies, waits for them, and re-layouts  18.3 us (10%)
  between operations  15.8 us (8%)
  other arithmetic  13.8 us (7%)
  matrix products  6.34 us (3%)
    psum x1, waiting for transfers between devices, body(): sums = lax.psum(partial_sums, ('blk', 'span'))  47.2 us
    ppermute x8, starting transfers between devices, passed_along(): lax.ppermute(value, axis, [(source, source + steps) for source in range(f...  24.3 us
    ppermute x8, waiting for transfers between devices, passed_along(): lax.ppermute(value, axis, [(source, source + steps) for source in range(f...  18.2 us
    all_to_all x1, waiting for transfers between devices, body(): lax.all_to_all(send_rows.reshape(owners, capacity, width), 'blk', split_a...  16.9 us
    all_to_all x1, starting transfers between devices, body(): lax.all_to_all(send_rows.reshape(owners, capacity, width), 'blk', split_a...  7.31 us
    all_to_all x1, starting transfers between devices, body(): lax.all_to_all(best.reshape(owners, capacity), 'blk', split_axis=0, conca...  5.92 us
    scatter x1, local copies, waits for them, and re-layouts, body(): jnp.zeros((share_limit, width), jnp.bfloat16).at[target]  5.74 us
    all_to_all x1, waiting for transfers between devices, body(): lax.all_to_all(best.reshape(owners, capacity), 'blk', split_axis=0, conca...  5.68 us
  transfers between devices with their start and end apart: 13, of which 7 were waited for; matrix products, arithmetic and copies ran while one was open for 13% of the time, Pallas kernels for 0%

commit v1 on v0

v1 whole, which is shorter than its diff:
```python
import jax
import jax.numpy as jnp
from jax import lax
from jax.experimental import pallas as pl
from jax.experimental.pallas import tpu as pltpu
from jax.sharding import PartitionSpec as P

F32 = jnp.float32
BF16 = jnp.bfloat16
I32 = jnp.int32
NT = (((1,), (1,)), ((), ()))


class Sizes:
    def __init__(self, owners, rows, width, clusters):
        self.owners, self.rows, self.width = owners, rows, width
        self.owned = clusters // owners
        self.own = 2 * rows // owners
        self.help = -(-(self.own // 4) // 8) * 8
        self.block = self.own + self.help + 8
        self.n_own = owners * self.own
        self.n_help = owners * self.help
        self.lanes = self.n_own + self.n_help
        assert owners & (owners - 1) == 0 and self.lanes <= width


def iota(shape, axis):
    return lax.broadcasted_iota(I32, shape, axis)


def dot(left, right):
    return jnp.dot(left, right, preferred_element_type=F32)


def dot_nt(left, right):
    return lax.dot_general(left, right, NT, preferred_element_type=F32)


def shared_heads(z, map_ref):
    return [map_ref[o * z.owned] for o in range(z.owners)]


def column(z, values):
    index = iota((z.owners, 1), 0)
    out = jnp.zeros((z.owners, 1), I32)
    for o, value in enumerate(values):
        out = jnp.where(index == o, value, out)
    return out


def pack_kernel(z, map_ref, x_ref, owner_ref, local_ref, info_ref, *out_refs):
    me = lax.axis_index("blk")
    wide = x_ref[...].astype(F32)
    scale = lax.rsqrt(jnp.sum(wide * wide, axis=1, keepdims=True) + 1e-06)
    unit = (wide * scale).astype(BF16)
    owner = owner_ref[...]
    local = local_ref[...]
    shape = (z.owners, z.rows)
    named = iota(shape, 0) == owner
    shared = named & (local == 0)
    heads = shared_heads(z, map_ref)
    helpers = []
    for o in range(z.owners):
        helper = jnp.int32(0)
        if o >= 2:
            helper = jnp.where(heads[o - 2] == heads[o], o - 2 + 1, helper)
        if o + 1 < z.owners:
            helper = jnp.where(heads[o + 1] == heads[o], o + 1 + 1, helper)
        helpers.append(helper)
    helper = jnp.sum(jnp.where(shared, column(z, helpers), 0), axis=0, keepdims=True)
    earlier = (iota((z.rows, z.rows), 0) < iota((z.rows, z.rows), 1)).astype(F32).astype(BF16)
    both = jnp.concatenate([named.astype(F32), shared.astype(F32)], axis=0).astype(BF16)
    before = dot(both, earlier)
    rank = jnp.sum(jnp.where(named, before[: z.owners], 0.0), axis=0, keepdims=True).astype(I32)
    rank0 = jnp.sum(jnp.where(shared, before[z.owners :], 0.0), axis=0, keepdims=True).astype(I32)
    rel = owner ^ me
    hrel = jnp.where(helper > 0, (helper - 1) ^ me, -1)
    pos = rel * z.block + rank
    hpos = jnp.where(helper > 0, hrel * z.block + z.own + rank0, -1)
    slot = iota((z.owners * z.block, z.rows), 0)
    pick = jnp.where((slot == pos) | (slot == hpos), 1.0, 0.0).astype(BF16)
    packed = dot(pick, unit).astype(BF16)
    tpos = rel * z.own + rank
    thpos = jnp.where(helper > 0, z.n_own + hrel * z.help + rank0, -1)
    lane = iota((z.lanes, z.rows), 0)
    pick_tag = jnp.where((lane == tpos) | (lane == thpos), 1.0, 0.0).astype(BF16)
    weight = jnp.where(iota(shape, 0) == rel, local + 1, 0).astype(F32).astype(BF16)
    helped = jnp.where(iota(shape, 0) == hrel, 1.0, 0.0).astype(BF16)
    tags = jnp.concatenate(
        [dot_nt(weight, pick_tag[: z.n_own]), dot_nt(helped, pick_tag[z.n_own :])], axis=1
    )
    filled = jnp.zeros((8, z.width - z.lanes), BF16) if z.width > z.lanes else None
    for s in range(z.owners):
        out = out_refs[s]
        out[: z.block - 8, :] = packed[s * z.block : (s + 1) * z.block - 8]
        out[z.block - 8 :, : z.lanes] = jnp.broadcast_to(tags[s : s + 1], (8, z.lanes)).astype(BF16)
        if filled is not None:
            out[z.block - 8 :, z.lanes :] = filled
    info = jnp.concatenate([pos * 0 + tpos, helper, thpos, local], axis=0)
    info_ref[...] = jnp.concatenate([info, info], axis=0)


def score_kernel(z, *refs):
    mine, other = refs[: z.owners], refs[z.owners : 2 * z.owners]
    ret_ref, own_ref, help_ref = refs[2 * z.owners :]
    me = lax.axis_index("blk")
    tags = []
    for half, blocks in enumerate((mine, other)):
        total = jnp.zeros((8, z.lanes), F32)
        for s, block in enumerate(blocks):
            own_ref[pl.ds(half * z.n_own + s * z.own, z.own), :] = block[: z.own, :]
            help_ref[pl.ds(half * z.n_help + s * z.help, z.help), :] = block[z.own : z.own + z.help, :]
            total += block[z.own + z.help :, : z.lanes].astype(F32)
        tags.append(total[:1])
    own_row = jnp.concatenate([t[:, : z.n_own] for t in tags], axis=1)
    help_row = jnp.concatenate([t[:, z.n_own :] for t in tags], axis=1)

    def columns(row):
        pieces = [row[:, i : i + 128] for i in range(0, row.shape[1], 128)]
        while len(pieces) < 8:
            pieces.append(jnp.zeros((1, 128), F32))
        return jnp.concatenate(pieces, axis=0).T

    own_cols, help_cols = columns(own_row), columns(help_row)
    my_own = jnp.where(own_row[:, : z.n_own] > 0, own_row[:, : z.n_own], -1.0)
    my_help = jnp.where(help_row[:, : z.n_help] > 0, help_row[:, : z.n_help], -1.0)
    rows_own = own_ref[: z.n_own, :]
    rows_help = help_ref[: z.n_help, :]

    def masked(keys, cols, first, rows, row_tags, skip_self):
        scores = dot_nt(keys, rows)
        best = None
        for q in range(keys.shape[0] // 128):
            piece = scores[q * 128 : (q + 1) * 128]
            keep = cols[:, first + q : first + q + 1] == row_tags
            if skip_self:
                keep &= iota(piece.shape, 0) + q * 128 != iota(piece.shape, 1)
            piece = jnp.where(keep, piece, -1.0)
            piece = jnp.max(piece.reshape(16, 8, piece.shape[1]), axis=0)
            best = piece if best is None else jnp.maximum(best, piece)
        return best

    half = z.n_own // 128
    keys0, keys1 = own_ref[: z.n_own, :], own_ref[z.n_own :, :]
    best_own = jnp.maximum(
        masked(keys0, own_cols, 0, rows_own, my_own, True),
        masked(keys1, own_cols, half, rows_own, my_own, False),
    )
    best_own = jnp.maximum(best_own, masked(help_ref[...], help_cols, 0, rows_own, my_own, False))
    best_help = jnp.maximum(
        masked(keys0, own_cols, 0, rows_help, my_help, False),
        masked(keys1, own_cols, half, rows_help, my_help, False),
    )
    best_own = jnp.max(best_own, axis=0, keepdims=True)
    best_help = jnp.max(best_help, axis=0, keepdims=True)

    owned = z.owned
    chosen = (iota((owned, 2 * z.n_own), 0) + 1).astype(F32) == own_row
    sums = dot(jnp.where(chosen, 1.0, 0.0).astype(BF16), own_ref[...])
    helped = (iota((owned, 2 * z.n_help), 0) + 1).astype(F32) == help_row
    extra = dot(jnp.where(helped, 1.0, 0.0).astype(BF16), help_ref[...])
    square = jnp.sum(sums * (sums + 2.0 * extra), axis=1, keepdims=True)
    inverse = 1.0 / jnp.maximum(jnp.sqrt(jnp.maximum(square, 0.0)), 1.0)
    inverse = jnp.where(iota((owned, 1), 0) == 0, 1.0, inverse)
    both = jnp.concatenate([sums + extra, sums], axis=0)
    high = both.astype(BF16)
    low = (both - high.astype(F32)).astype(BF16)
    parts = jnp.concatenate([high, low], axis=0)
    along = dot_nt(parts, rows_own)
    along = (along[:owned] + along[2 * owned : 3 * owned]) * inverse
    hits = (iota((owned, z.n_own), 0) + 1).astype(F32) == my_own
    value_own = jnp.sum(jnp.where(hits, along, 0.0), axis=0, keepdims=True)
    along = dot_nt(parts, rows_help)
    value_help = along[owned : owned + 1] + along[3 * owned : 3 * owned + 1]
    shared_square = jnp.broadcast_to(square[:1], (1, 128))
    for s in range(z.owners):
        o = s * z.own // 128 * 128
        h = s * z.help // 128 * 128
        parts = [
            best_own[:, o : o + 128],
            best_help[:, h : h + 128],
            value_own[:, o : o + 128],
            value_help[:, h : h + 128],
        ] + [shared_square] * 4
        ret_ref[me ^ s] = jnp.concatenate(parts, axis=0)


def finish_kernel(z, map_ref, ret_ref, info_ref, owner_ref, nearest_ref, cosine_ref):
    owner = owner_ref[...]
    tpos, helper, thpos, local = (info_ref[i : i + 1, :] for i in range(4))
    back = ret_ref[...].reshape(z.owners * 8, 128).T
    slot = iota((128, z.rows), 0)
    own_slot = jnp.where(slot == tpos % 128, owner, -1)
    help_slot = jnp.where(slot == thpos % 128, helper - 1, -1)
    best = jnp.full((128, z.rows), -1.0, F32)
    value = jnp.zeros((128, z.rows), F32)
    for d in range(z.owners):
        mine = own_slot == d
        extra = help_slot == d
        best = jnp.maximum(best, jnp.where(mine, back[:, 8 * d : 8 * d + 1], -1.0))
        best = jnp.maximum(best, jnp.where(extra, back[:, 8 * d + 1 : 8 * d + 2], -1.0))
        value += jnp.where(mine, back[:, 8 * d + 2 : 8 * d + 3], 0.0)
        value += jnp.where(extra, back[:, 8 * d + 3 : 8 * d + 4], 0.0)
    best = jnp.max(best, axis=0, keepdims=True)
    value = jnp.sum(value, axis=0, keepdims=True)
    heads = column(z, shared_heads(z, map_ref))
    named = iota((z.owners, z.rows), 0) == owner
    head = jnp.sum(jnp.where(named, heads, 0), axis=0, keepdims=True)
    squares = ret_ref[:, 4, :][:, :1]
    square = jnp.sum(jnp.where(heads == head, squares, 0.0), axis=0, keepdims=True)
    shared = value / jnp.maximum(jnp.sqrt(jnp.maximum(square, 0.0)), 1.0)
    nearest_ref[...] = best
    cosine_ref[...] = jnp.where(local == 0, shared, value)


def body(embeddings, owner_ids, local_ids, cluster_map):
    rows, width = embeddings.shape
    n = lax.axis_size("blk")
    z = Sizes(n, rows, width, cluster_map.shape[0])
    vmem = pl.BlockSpec(memory_space=pltpu.VMEM)
    smem = pl.BlockSpec(memory_space=pltpu.SMEM)
    owner = owner_ids.reshape(1, rows)
    local = local_ids.reshape(1, rows)
    block = jax.ShapeDtypeStruct((z.block, width), BF16)
    limit = pltpu.CompilerParams(vmem_limit_bytes=24 * 2**20)
    packed = pl.pallas_call(
        lambda *refs: pack_kernel(z, *refs),
        out_shape=[jax.ShapeDtypeStruct((8, rows), I32)] + [block] * n,
        in_specs=[smem, vmem, vmem, vmem],
        out_specs=[vmem] * (n + 1),
        compiler_params=limit,
        name="pack",
    )(cluster_map, embeddings, owner, local)
    info, blocks = packed[0], packed[1:]
    swap = [(0, 1), (1, 0)]
    order = sorted(range(1, n), key=lambda s: -(s.bit_length()))
    mine = {0: blocks[0]}
    for s in order:
        mine[s] = lax.ppermute(blocks[s], "blk", [(i, i ^ s) for i in range(n)])
    other = {s: lax.ppermute(mine[s], "span", swap) for s in range(n)}
    ret = pl.pallas_call(
        lambda *refs: score_kernel(z, *refs),
        out_shape=jax.ShapeDtypeStruct((n, 8, 128), F32),
        in_specs=[vmem] * (2 * n),
        out_specs=vmem,
        scratch_shapes=[
            pltpu.VMEM((2 * z.n_own, width), BF16),
            pltpu.VMEM((2 * z.n_help, width), BF16),
        ],
        compiler_params=limit,
        name="score",
    )(*[mine[s] for s in range(n)], *[other[s] for s in range(n)])
    back = lax.all_to_all(ret, "blk", split_axis=0, concat_axis=0, tiled=True)
    row = jax.ShapeDtypeStruct((1, rows), F32)
    nearest, cosine = pl.pallas_call(
        lambda *refs: finish_kernel(z, *refs),
        out_shape=[row, row],
        in_specs=[smem, vmem, vmem, vmem],
        out_specs=[vmem, vmem],
        compiler_params=limit,
        name="finish",
    )(cluster_map, back, info, owner)
    return nearest.reshape(rows), cosine.reshape(rows)


def solution(mesh):
    return jax.shard_map(
        body,
        mesh=mesh,
        in_specs=(
            P(("groups", "blk", "span"), None),
            P(("groups", "blk", "span"), None),
            P(("groups", "blk", "span")),
            P("groups"),
        ),
        out_specs=(P(("groups", "blk", "span")), P(("groups", "blk", "span"))),
        check_vma=False,
    )
```

time: 192 us -> 52.2 us (0.27)
  waiting for transfers between devices: 93.8 us -> 15.2 us
  starting transfers between devices: 41.1 us -> 15 us
  local copies, waits for them, and re-layouts: 18.3 us -> 1.67 us
  between operations: 15.8 us -> 0.69 us
  other arithmetic: 13.8 us -> 0 us
  blocking collectives: 1.83 us -> 13.9 us
  matrix products: 6.34 us -> 0 us
  Pallas kernels: 0 us -> 5.44 us
    psum x1 -> x0, waiting for transfers between devices: 47.2 us -> none  [body(): sums = lax.psum(partial_sums, ('blk', 'span'))]
    all_to_all x3 -> x0, waiting for transfers between devices: 27.8 us -> none  [the longest x1 16.9 us: body(): lax.all_to_all(send_rows.reshape(owners, capacity, width), 'blk', split_a...]
    all_to_all x3 -> x0, starting transfers between devices: 16.7 us -> none  [the longest x1 7.31 us: body(): lax.all_to_all(send_rows.reshape(owners, capacity, width), 'blk', split_a...]
    all_to_all x0 -> x1, blocking collectives: none -> 13.9 us  [body(): back = lax.all_to_all(ret, 'blk', split_axis=0, concat_axis=0, tiled=True)]
    scatter x3 -> x0, local copies, waits for them, and re-layouts: 11.4 us -> none  [the longest x1 5.74 us: body(): jnp.zeros((share_limit, width), jnp.bfloat16).at[target]]
    ppermute x8 -> x15, starting transfers between devices: 24.3 us -> 15 us  [the longest x7 13.2 us: body(): mine[s] = lax.ppermute(blocks[s], 'blk', [(i, i ^ s) for i in range(n)])]
    dot_general x6 -> x0, matrix products: 6.34 us -> none  [the longest x5 5.24 us: masked_scores(): lax.dot_general(left, right, (((1,), (1,)), ((), ())), preferred_element_...]
    pallas_call x0 -> x3, Pallas kernels: none -> 5.44 us  [the longest x1 2.22 us: body(): pl.pallas_call(lambda *refs: score_kernel(z, *refs), out_shape=jax.ShapeD...]
  transfers between devices with their start and end apart: 13 -> 15, of which waited for: 7 -> 7; matrix products, arithmetic and copies ran while one was open for 13% -> 0% of each run, Pallas kernels for 0% -> 0%
where the time goes in v1:
time: 52.2 us; the launch traced here: 51.9 us
  waiting for transfers between devices  15.2 us (29%)
  starting transfers between devices  15 us (29%)
  blocking collectives  13.9 us (27%)
  Pallas kernels  5.44 us (10%)
  local copies, waits for them, and re-layouts  1.67 us (3%)
  between operations  0.69 us (1%)
    all_to_all x1, blocking collectives, body(): back = lax.all_to_all(ret, 'blk', split_axis=0, concat_axis=0, tiled=True)  13.9 us
    ppermute x7, waiting for transfers between devices, body(): mine[s] = lax.ppermute(blocks[s], 'blk', [(i, i ^ s) for i in range(n)])  13.8 us
    ppermute x7, starting transfers between devices, body(): mine[s] = lax.ppermute(blocks[s], 'blk', [(i, i ^ s) for i in range(n)])  13.2 us
    pallas_call x1, Pallas kernels, body(): pl.pallas_call(lambda *refs: score_kernel(z, *refs), out_shape=jax.ShapeD...  2.22 us
    pallas_call x1, Pallas kernels, body(): pl.pallas_call(lambda *refs: finish_kernel(z, *refs), out_shape=[row, row...  1.91 us
    ppermute x8, starting transfers between devices, body(): other = {s: lax.ppermute(mine[s], 'span', swap) for s in range(n)}  1.8 us
    unnamed x8, local copies, waits for them, and re-layouts  1.67 us
    ppermute x8, waiting for transfers between devices, body(): other = {s: lax.ppermute(mine[s], 'span', swap) for s in range(n)}  1.41 us
  transfers between devices with their start and end apart: 15, of which 7 were waited for; matrix products, arithmetic and copies ran while one was open for 0% of the time, Pallas kernels for 0%

profile of v1, /device:TPU:0, one launch (start us, length us, event | category | flops | bytes accessed | tf_op | source)
XLA Modules:
  0.0 51.9 jit_solution(11200518451247126749)
XLA Ops:
  0.7 0.7 %copy-done.3 = s32[256]{0:T(256)S(1)} copy-done((s32[256]{0:T(256)S(1)}, s32[256]{0:T(256)}, u32[]{:S(2)}) %copy-start.3) | copy-done | bytes 1048
  1.3 0.0 copy-done.1
  1.3 1.0 %copy-done = bf16[256,768]{1,0:T(8,128)(2,1)S(1)} copy-done((bf16[256,768]{1,0:T(8,128)(2,1)S(1)}, bf16[256,768]{1,0:T(8,128)(2,1)}, u32[]{:S(2)}) %copy-start) | copy-done | bytes 393240
  2.3 1.3 %pack.1 = (s32[8,256]{1,0:T(8,128)S(1)}, bf16[88,768]{1,0:T(8,128)(2,1)S(1)}, bf16[88,768]{1,0:T(8,128)(2,1)S(1)}, bf16[88,768]{1,0:T(8,128)(2,1)S(1)}, bf16[88,...) custom-call(s32[128]{0:T(128)S(1)} %copy-done.2, ...), custom_call_target="tpu_custom_call" | custom-call | tf_op jit(solution)/shard_map/pack/pallas_call | solution.py:226
  3.6 3.1 %collective-permute-start = (bf16[88,768]{1,0:T(8,128)(2,1)S(1)}, bf16[88,768]{1,0:T(8,128)(2,1)S(1)}, u32[]{:S(2)}, u32[]{:S(2)}) collective-permute-start(bf16[88,768]{1,0:T(8,128)(2,1)S(1)} %get-tuple-element.14), channel_id=1, source_target_pairs={{0,2},{2,0},{4,6},{6,4},{8,10},{10,8},{12,14},{14,12},{1,3},{3,1},... | collective-permute-start | bytes 405512 | tf_op jit(solution)/shard_map/ppermute | solution.py:239
  6.7 1.6 %collective-permute-start.1 = (bf16[88,768]{1,0:T(8,128)(2,1)S(1)}, bf16[88,768]{1,0:T(8,128)(2,1)S(1)}, u32[]{:S(2)}, u32[]{:S(2)}) collective-permute-start(bf16[88,768]{1,0:T(8,128)(2,1)S(1)} %get-tuple-element.15), channel_id=1, source_target_pairs={{0,4},{2,6},{4,0},{6,2},{8,12},{10,14},{12,8},{14,10},{1,5},{3,7},... | collective-permute-start | bytes 405512 | tf_op jit(solution)/shard_map/ppermute | solution.py:239
  8.3 0.0 collective-permute-start.2
  8.3 3.0 %collective-permute-start.3 = (bf16[88,768]{1,0:T(8,128)(2,1)S(1)}, bf16[88,768]{1,0:T(8,128)(2,1)S(1)}, u32[]{:S(2)}, u32[]{:S(2)}) collective-permute-start(bf16[88,768]{1,0:T(8,128)(2,1)S(1)} %get-tuple-element.17), channel_id=1, source_target_pairs={{0,8},{2,10},{4,12},{6,14},{8,0},{10,2},{12,4},{14,6},{1,9},{3,11}... | collective-permute-start | bytes 405512 | tf_op jit(solution)/shard_map/ppermute | solution.py:239
  11.3 1.3 %collective-permute-start.4 = (bf16[88,768]{1,0:T(8,128)(2,1)S(1)}, bf16[88,768]{1,0:T(8,128)(2,1)S(1)}, u32[]{:S(2)}, u32[]{:S(2)}) collective-permute-start(bf16[88,768]{1,0:T(8,128)(2,1)S(1)} %get-tuple-element.18), channel_id=1, source_target_pairs={{0,10},{2,8},{4,14},{6,12},{8,2},{10,0},{12,6},{14,4},{1,11},{3,9}... | collective-permute-start | bytes 405512 | tf_op jit(solution)/shard_map/ppermute | solution.py:239
  12.6 0.0 collective-permute-done.refs_1_
  12.6 3.6 %collective-permute-start.5 = (bf16[88,768]{1,0:T(8,128)(2,1)S(1)}, bf16[88,768]{1,0:T(8,128)(2,1)S(1)}, u32[]{:S(2)}, u32[]{:S(2)}) collective-permute-start(bf16[88,768]{1,0:T(8,128)(2,1)S(1)} %get-tuple-element.19), channel_id=1, source_target_pairs={{0,12},{2,14},{4,8},{6,10},{8,4},{10,6},{12,0},{14,2},{1,13},{3,15... | collective-permute-start | bytes 405512 | tf_op jit(solution)/shard_map/ppermute | solution.py:239
  16.2 1.6 %collective-permute-done.1.refs_2_ = bf16[88,768]{1,0:T(8,128)(2,1)S(1)} collective-permute-done((bf16[88,768]{1,0:T(8,128)(2,1)S(1)}, bf16[88,768]{1,0:T(8,128)(2,1)S(1)}, u32[]{:S(2)}, u32[]{:S(2)}) %collective-permute-start.1) | collective-permute-done | bytes 135200 | tf_op jit(solution)/shard_map/ppermute | solution.py:239
  17.8 0.7 %collective-permute-start.6 = (bf16[88,768]{1,0:T(8,128)(2,1)S(1)}, bf16[88,768]{1,0:T(8,128)(2,1)S(1)}, u32[]{:S(2)}, u32[]{:S(2)}) collective-permute-start(bf16[88,768]{1,0:T(8,128)(2,1)S(1)} %get-tuple-element.20), channel_id=1, source_target_pairs={{0,14},{2,12},{4,10},{6,8},{8,6},{10,4},{12,2},{14,0},{1,15},{3,13... | collective-permute-start | bytes 405512 | tf_op jit(solution)/shard_map/ppermute | solution.py:239
  18.5 0.0 collective-permute-done.2.refs_3_
  18.5 0.0 collective-permute-start.7
  18.5 0.5 collective-permute-start.8
  19.0 12.2 %collective-permute-done.4.refs_5_ = bf16[88,768]{1,0:T(8,128)(2,1)S(1)} collective-permute-done((bf16[88,768]{1,0:T(8,128)(2,1)S(1)}, bf16[88,768]{1,0:T(8,128)(2,1)S(1)}, u32[]{:S(2)}, u32[]{:S(2)}) %collective-permute-start.4) | collective-permute-done | bytes 135200 | tf_op jit(solution)/shard_map/ppermute | solution.py:239
  31.2 0.0 collective-permute-start.9
  31.2 0.0 collective-permute-done.5.refs_6_
  31.2 0.5 collective-permute-start.10
  31.8 0.1 collective-permute-start.11
  31.8 0.4 collective-permute-start.12
  32.3 0.1 collective-permute-start.13
  32.3 0.2 collective-permute-done.9.refs_10_
  32.6 0.2 collective-permute-start.14
  32.8 0.3 collective-permute-done.11.refs_12_
  33.1 0.2 collective-permute-done.12.refs_13_
  33.3 0.3 collective-permute-done.13.refs_14_
  33.6 0.3 collective-permute-done.14.refs_15_
  33.9 2.2 %score.1 = f32[8,8,128]{2,1,0:T(8,128)S(1)} custom-call(bf16[88,768]{1,0:T(8,128)(2,1)S(1)} %get-tuple-element.13.refs_0_, bf16[88,768]{1,0:T(8,128)(2,1)S(1)} %collective-permute-done.refs_1_, bf16[88,768]{1,0:T(8,128)(2,1)S(1)} %collective-permute-done.1.refs_2_, bf16[88,768]{1,0:T(8,128)(2,1)S(1)} %collective-permute-done.2.refs_3_, ...), custom_call_target="tpu_custom_call" | custom-call | tf_op jit(solution)/shard_map/score/pallas_call | solution.py:241
  36.2 13.9 %all_to_all.5.refs_1_ = f32[8,8,128]{2,1,0:T(8,128)S(1)} all-to-all(f32[8,8,128]{2,1,0:T(8,128)S(1)} %score.1), channel_id=1, replica_groups=mesh['groups'=2,'blk'=8,'span'=2] {'blk'}, dimensions={0} | all-to-all | bytes 65536 | tf_op jit(solution)/shard_map/all_to_all | solution.py:253
  50.0 1.9 %finish.1 = (f32[1,256]{1,0:T(1,128)}, f32[1,256]{1,0:T(1,128)}) custom-call(s32[128]{0:T(128)S(1)} %copy-done.2, f32[8,8,128]{2,1,0:T(8,128)S(1)} %all_to_all.5.refs_1_, s32[8,256]{1,0:T(8,128)S(1)} %get-tuple-element.21.refs_2_, s32[1,256]{1,0:T(1,128)S(1)} %bitcast.5), custom_call_target="tpu_custom_call" | custom-call | tf_op jit(solution)/shard_map/finish/pallas_call | solution.py:255
  (10 shorter events, 0.0 us)
Async XLA Ops:
  0.6 0.7 %copy-start.3 = (s32[256]{0:T(256)S(1)}, s32[256]{0:T(256)}, u32[]{:S(2)}) copy-start(s32[256]{0:T(256)} %param.6) | copy-start | bytes 3076
  0.6 0.7 %copy-start.1 = (s32[256,1]{0,1:T(1,128)S(1)}, s32[256,1]{0,1:T(1,128)}, u32[]{:S(2)}) copy-start(s32[256,1]{0,1:T(1,128)} %param.5) | copy-start | bytes 3076
  0.7 0.7 %copy-start.2 = (s32[128]{0:T(128)S(1)}, s32[128]{0:T(128)}, u32[]{:S(2)}) copy-start(s32[128]{0:T(128)} %refs_0_.3) | copy-start | bytes 1540
  1.3 1.0 %copy-start = (bf16[256,768]{1,0:T(8,128)(2,1)S(1)}, bf16[256,768]{1,0:T(8,128)(2,1)}, u32[]{:S(2)}) copy-start(bf16[256,768]{1,0:T(8,128)(2,1)} %refs_1_.1) | copy-start | bytes 1179652
  3.6 8.9 %collective-permute-start = (bf16[88,768]{1,0:T(8,128)(2,1)S(1)}, bf16[88,768]{1,0:T(8,128)(2,1)S(1)}, u32[]{:S(2)}, u32[]{:S(2)}) collective-permute-start(bf16[88,768]{1,0:T(8,128)(2,1)S(1)} %get-tuple-element.14), channel_id=1, source_target_pairs={{0,2},{2,0},{4,6},{6,4},{8,10},{10,8},{12,14},{14,12},{1,3},{3,1},... | collective-permute-start | bytes 405512 | tf_op jit(solution)/shard_map/ppermute | solution.py:239
  6.7 11.1 %collective-permute-start.1 = (bf16[88,768]{1,0:T(8,128)(2,1)S(1)}, bf16[88,768]{1,0:T(8,128)(2,1)S(1)}, u32[]{:S(2)}, u32[]{:S(2)}) collective-permute-start(bf16[88,768]{1,0:T(8,128)(2,1)S(1)} %get-tuple-element.15), channel_id=1, source_target_pairs={{0,4},{2,6},{4,0},{6,2},{8,12},{10,14},{12,8},{14,10},{1,5},{3,7},... | collective-permute-start | bytes 405512 | tf_op jit(solution)/shard_map/ppermute | solution.py:239
  8.3 10.2 %collective-permute-start.2 = (bf16[88,768]{1,0:T(8,128)(2,1)S(1)}, bf16[88,768]{1,0:T(8,128)(2,1)S(1)}, u32[]{:S(2)}, u32[]{:S(2)}) collective-permute-start(bf16[88,768]{1,0:T(8,128)(2,1)S(1)} %get-tuple-element.16), channel_id=1, source_target_pairs={{0,6},{2,4},{4,2},{6,0},{8,14},{10,12},{12,10},{14,8},{1,7},{3,5},... | collective-permute-start | bytes 405512 | tf_op jit(solution)/shard_map/ppermute | solution.py:239
  8.3 10.2 %collective-permute-start.3 = (bf16[88,768]{1,0:T(8,128)(2,1)S(1)}, bf16[88,768]{1,0:T(8,128)(2,1)S(1)}, u32[]{:S(2)}, u32[]{:S(2)}) collective-permute-start(bf16[88,768]{1,0:T(8,128)(2,1)S(1)} %get-tuple-element.17), channel_id=1, source_target_pairs={{0,8},{2,10},{4,12},{6,14},{8,0},{10,2},{12,4},{14,6},{1,9},{3,11}... | collective-permute-start | bytes 405512 | tf_op jit(solution)/shard_map/ppermute | solution.py:239
  11.3 20.0 %collective-permute-start.4 = (bf16[88,768]{1,0:T(8,128)(2,1)S(1)}, bf16[88,768]{1,0:T(8,128)(2,1)S(1)}, u32[]{:S(2)}, u32[]{:S(2)}) collective-permute-start(bf16[88,768]{1,0:T(8,128)(2,1)S(1)} %get-tuple-element.18), channel_id=1, source_target_pairs={{0,10},{2,8},{4,14},{6,12},{8,2},{10,0},{12,6},{14,4},{1,11},{3,9}... | collective-permute-start | bytes 405512 | tf_op jit(solution)/shard_map/ppermute | solution.py:239
  12.6 18.7 %collective-permute-start.5 = (bf16[88,768]{1,0:T(8,128)(2,1)S(1)}, bf16[88,768]{1,0:T(8,128)(2,1)S(1)}, u32[]{:S(2)}, u32[]{:S(2)}) collective-permute-start(bf16[88,768]{1,0:T(8,128)(2,1)S(1)} %get-tuple-element.19), channel_id=1, source_target_pairs={{0,12},{2,14},{4,8},{6,10},{8,4},{10,6},{12,0},{14,2},{1,13},{3,15... | collective-permute-start | bytes 405512 | tf_op jit(solution)/shard_map/ppermute | solution.py:239
  17.8 14.0 %collective-permute-start.6 = (bf16[88,768]{1,0:T(8,128)(2,1)S(1)}, bf16[88,768]{1,0:T(8,128)(2,1)S(1)}, u32[]{:S(2)}, u32[]{:S(2)}) collective-permute-start(bf16[88,768]{1,0:T(8,128)(2,1)S(1)} %get-tuple-element.20), channel_id=1, source_target_pairs={{0,14},{2,12},{4,10},{6,8},{8,6},{10,4},{12,2},{14,0},{1,15},{3,13... | collective-permute-start | bytes 405512 | tf_op jit(solution)/shard_map/ppermute | solution.py:239
  18.5 13.3 %collective-permute-start.7 = (bf16[88,768]{1,0:T(8,128)(2,1)S(1)}, bf16[88,768]{1,0:T(8,128)(2,1)S(1)}, u32[]{:S(2)}, u32[]{:S(2)}) collective-permute-start(bf16[88,768]{1,0:T(8,128)(2,1)S(1)} %get-tuple-element.13.refs_0_), channel_id=1, source_target_pairs={{0,1},{1,0},{2,3},{3,2},{4,5},{5,4},{6,7},{7,6},{8,9},{9,8},{10,11... | collective-permute-start | bytes 405512 | tf_op jit(solution)/shard_map/ppermute | solution.py:240
  18.5 13.7 %collective-permute-start.8 = (bf16[88,768]{1,0:T(8,128)(2,1)S(1)}, bf16[88,768]{1,0:T(8,128)(2,1)S(1)}, u32[]{:S(2)}, u32[]{:S(2)}) collective-permute-start(bf16[88,768]{1,0:T(8,128)(2,1)S(1)} %collective-permute-done.refs_1_), channel_id=1, source_target_pairs={{0,1},{1,0},{2,3},{3,2},{4,5},{5,4},{6,7},{7,6},{8,9},{9,8},{10,11... | collective-permute-start | bytes 405512 | tf_op jit(solution)/shard_map/ppermute | solution.py:240
  31.2 1.4 %collective-permute-start.9 = (bf16[88,768]{1,0:T(8,128)(2,1)S(1)}, bf16[88,768]{1,0:T(8,128)(2,1)S(1)}, u32[]{:S(2)}, u32[]{:S(2)}) collective-permute-start(bf16[88,768]{1,0:T(8,128)(2,1)S(1)} %collective-permute-done.1.refs_2_), channel_id=1, source_target_pairs={{0,1},{1,0},{2,3},{3,2},{4,5},{5,4},{6,7},{7,6},{8,9},{9,8},{10,11... | collective-permute-start | bytes 405512 | tf_op jit(solution)/shard_map/ppermute | solution.py:240
  31.2 1.5 %collective-permute-start.10 = (bf16[88,768]{1,0:T(8,128)(2,1)S(1)}, bf16[88,768]{1,0:T(8,128)(2,1)S(1)}, u32[]{:S(2)}, u32[]{:S(2)}) collective-permute-start(bf16[88,768]{1,0:T(8,128)(2,1)S(1)} %collective-permute-done.2.refs_3_), channel_id=1, source_target_pairs={{0,1},{1,0},{2,3},{3,2},{4,5},{5,4},{6,7},{7,6},{8,9},{9,8},{10,11... | collective-permute-start | bytes 405512 | tf_op jit(solution)/shard_map/ppermute | solution.py:240
  31.8 1.4 %collective-permute-start.11 = (bf16[88,768]{1,0:T(8,128)(2,1)S(1)}, bf16[88,768]{1,0:T(8,128)(2,1)S(1)}, u32[]{:S(2)}, u32[]{:S(2)}) collective-permute-start(bf16[88,768]{1,0:T(8,128)(2,1)S(1)} %collective-permute-done.3.refs_4_), channel_id=1, source_target_pairs={{0,1},{1,0},{2,3},{3,2},{4,5},{5,4},{6,7},{7,6},{8,9},{9,8},{10,11... | collective-permute-start | bytes 405512 | tf_op jit(solution)/shard_map/ppermute | solution.py:240
  31.8 1.5 %collective-permute-start.12 = (bf16[88,768]{1,0:T(8,128)(2,1)S(1)}, bf16[88,768]{1,0:T(8,128)(2,1)S(1)}, u32[]{:S(2)}, u32[]{:S(2)}) collective-permute-start(bf16[88,768]{1,0:T(8,128)(2,1)S(1)} %collective-permute-done.4.refs_5_), channel_id=1, source_target_pairs={{0,1},{1,0},{2,3},{3,2},{4,5},{5,4},{6,7},{7,6},{8,9},{9,8},{10,11... | collective-permute-start | bytes 405512 | tf_op jit(solution)/shard_map/ppermute | solution.py:240
  32.3 1.4 %collective-permute-start.13 = (bf16[88,768]{1,0:T(8,128)(2,1)S(1)}, bf16[88,768]{1,0:T(8,128)(2,1)S(1)}, u32[]{:S(2)}, u32[]{:S(2)}) collective-permute-start(bf16[88,768]{1,0:T(8,128)(2,1)S(1)} %collective-permute-done.5.refs_6_), channel_id=1, source_target_pairs={{0,1},{1,0},{2,3},{3,2},{4,5},{5,4},{6,7},{7,6},{8,9},{9,8},{10,11... | collective-permute-start | bytes 405512 | tf_op jit(solution)/shard_map/ppermute | solution.py:240
  32.6 1.4 %collective-permute-start.14 = (bf16[88,768]{1,0:T(8,128)(2,1)S(1)}, bf16[88,768]{1,0:T(8,128)(2,1)S(1)}, u32[]{:S(2)}, u32[]{:S(2)}) collective-permute-start(bf16[88,768]{1,0:T(8,128)(2,1)S(1)} %collective-permute-done.6.refs_7_), channel_id=1, source_target_pairs={{0,1},{1,0},{2,3},{3,2},{4,5},{5,4},{6,7},{7,6},{8,9},{9,8},{10,11... | collective-permute-start | bytes 405512 | tf_op jit(solution)/shard_map/ppermute | solution.py:240
